TPU v7x, 256 devices: a whole 4x4x8 slice. The times are simulated.
256 devices in a mesh: seq: 32 (over x, z), batch: 8 (over y, core).
Axes of the slice: x: 4, y: 4, z: 8, core: 2. Of those that a mesh axis runs over, the one named last changes fastest.
Arguments:
- hidden: bfloat16 [16, 8192, 4096], P('batch', None, 'seq')
- gain: float32 [4096], P('seq'), may hold values from 0.5 to 1.5
- value_weight: float32 [4096], P('seq'), may hold values from -0.09375 to 0.09375
- rewards: float32 [16, 8192], P('batch', 'seq'), may hold values from -1.5 to 1.5
- reward_mask: int32 [16, 8192], P('batch', 'seq'), may hold values 0 or 1
- lengths: int32 [16], P('batch'), may hold values from 2048 to 8192
- horizon: float32 [16], P('batch'), may hold values from 24 to 65536
Outputs:
- advantages: float32 [16, 8192], P(None, ('seq', 'batch'))
- returns: float32 [16, 8192], P(None, ('seq', 'batch'))
All inputs are finite; a program needn't handle non-finite values. No bound on the sum of `reward_mask` on one device may be relied on, other than what follows from the above.
Results may differ from a plain program's by a relative error of at most 0.0003.
Values may be sent and summed in bfloat16 or wider, within the bound.
A program may use at most 64 MiB of HBM per device.

v0:
```python
import jax
import jax.numpy as jnp
from jax import lax
from jax.sharding import Mesh
from jax.sharding import PartitionSpec as P

D = 4096
SEQ = ("seq_0", "seq_1")
SEQ_BATCH = ("seq_0", "seq_1", "batch_0", "batch_1")
BATCH = ("batch_0", "batch_1")
EPS = 1e-05


def cut_along(array, dim, devices):
    dims = array.shape
    blocks = array.reshape(*dims[:dim], devices, dims[dim] // devices, *dims[dim + 1 :])
    return jnp.moveaxis(blocks, dim, 0)


def sent_and_summed(array, axis, dim):
    devices = lax.axis_size(axis)
    blocks = lax.all_to_all(cut_along(array, dim, devices), axis, 0, 0, tiled=True)
    return jnp.sum(blocks, axis=0)


def side_by_side(arrays, axis, dim, along):
    widths = [a.shape[along] for a in arrays]
    both = jnp.concatenate(arrays, axis=along)
    whole = sent_and_summed(both, axis, dim)
    return tuple(jnp.split(whole, [sum(widths[:k]) for k in range(1, len(widths))], axis=along))


def from_behind(value, axis, steps):
    count = lax.axis_size(axis)
    initial, last = (max(0, -steps), min(count, count - steps))
    return lax.ppermute(value, axis, [(source, source + steps) for source in range(initial, last)])


def sent_to_all(array, axis):
    devices = lax.axis_size(axis)
    return lax.all_to_all(
        jnp.broadcast_to(array[None], (devices, *array.shape)), axis, 0, 0, tiled=True
    )


def gathered_once(array, axis):
    leaves = jax.tree.leaves(array)
    turns = sorted(range(len(leaves)), key=lambda k: -leaves[k].size)
    width = (1, *leaves[turns[0]].shape)[-1]
    lines = [
        jnp.pad(leaves[k].reshape(-1), (0, -leaves[k].size % width)).reshape(-1, width)
        for k in turns
    ]
    both, at, found = (sent_to_all(jnp.concatenate(lines), axis), 0, {})
    for k, line in zip(turns, lines):
        slab = both[:, at : at + len(line)].reshape(len(both), -1)
        found[k] = slab[:, : leaves[k].size].reshape(-1, *leaves[k].shape)
        at += len(line)
    numbers = iter(range(len(leaves)))
    return jax.tree.map(lambda _: found[next(numbers)], array)


def joined_by_halves(pieces, combine):
    while len(jax.tree.leaves(pieces)[0]) > 1:
        pieces = jax.vmap(combine)(
            *(jax.tree.map(lambda part: part[side::2], pieces) for side in (0, 1))
        )
    return jax.tree.map(lambda part: part[0], pieces)


def prefix(array, axis, combine, identity):
    devices, position = (lax.axis_size(axis), lax.axis_index(axis))
    passed = jnp.arange(devices) > position

    def kept(part, zero, own):
        part = jnp.where(
            passed.reshape(-1, *(1 for _ in own.shape)), part, jnp.asarray(zero, own.dtype)
        )
        return part[::-1]

    pieces = gathered_once(array, axis)
    return joined_by_halves(jax.tree.map(kept, pieces, identity, array), combine)


def one_axis_at_a_time(array, axes):
    for axis in axes:
        array = lax.psum(array, axis)
    return array


def per_device(hidden, gain, value_weight, rewards, reward_mask, lengths, horizon):
    my_index = lax.axis_index(SEQ)
    block = rewards.shape[1]
    wide_rows = hidden.astype(jnp.float32)
    part_squares = jnp.sum(wide_rows * wide_rows, -1)
    part_projected = jnp.sum(wide_rows * (gain * value_weight), -1)
    squares, projected = side_by_side((part_squares, part_projected), SEQ, 1, 0)
    values = projected * lax.rsqrt(squares / D + EPS)
    positions = my_index * block + jnp.arange(block, dtype=jnp.int32)
    valid = (positions[None, :] < lengths[:, None]).astype(jnp.float32)
    next_valid = (positions[None, :] + 1 < lengths[:, None]).astype(jnp.float32)
    following = from_behind(values[:, 0], SEQ, -1)
    next_values = jnp.concatenate([values[:, 1:], following[:, None]], 1)
    delta = (rewards * reward_mask.astype(jnp.float32) + next_valid * next_values - values) * valid
    log_decay = -1.0 / horizon
    offsets = jnp.arange(block, dtype=jnp.int32)
    distance = (offsets[None, :] - offsets[:, None]).astype(jnp.float32)
    upper_mask = distance >= 0.0
    powers = jnp.where(
        upper_mask[None], jnp.exp(jnp.maximum(distance, 0.0)[None] * log_decay[:, None, None]), 0.0
    )
    local_gae = jnp.einsum("rtk,rk->rt", powers, delta, precision=lax.Precision.HIGHEST)
    tail_decay = jnp.exp((block - offsets).astype(jnp.float32)[None, :] * log_decay[:, None])
    start_value = local_gae[:, 0]
    block_decay = jnp.exp(block * log_decay)

    def compose(earlier, later):
        return (later[0] + later[1] * earlier[0], later[1] * earlier[1])

    carry_in, _ = prefix(
        (start_value, block_decay),
        SEQ,
        compose,
        (jnp.zeros_like(start_value), jnp.ones_like(block_decay)),
    )
    gae = local_gae + tail_decay * carry_in[:, None]
    returns = (gae + values) * valid
    count, first, second = (
        one_axis_at_a_time(jnp.sum(valid), SEQ_BATCH),
        one_axis_at_a_time(jnp.sum(gae), SEQ_BATCH),
        one_axis_at_a_time(jnp.sum(gae * gae), SEQ_BATCH),
    )
    mean = first / count
    var = jnp.maximum(second / count - mean * mean, 1.0)
    whitened = (gae - mean) * valid * lax.rsqrt(var)
    out_adv, out_returns = (
        lax.all_to_all(whitened, BATCH, split_axis=1, concat_axis=0, tiled=True),
        lax.all_to_all(returns, BATCH, split_axis=1, concat_axis=0, tiled=True),
    )
    return (out_adv, out_returns)


def solution(mesh):
    finer = Mesh(mesh.devices.reshape(4, 8, 4, 2), ("seq_0", "seq_1", "batch_0", "batch_1"))
    placed = (P(BATCH, None, SEQ), P(SEQ), P(SEQ), P(BATCH, SEQ), P(BATCH, SEQ), P(BATCH), P(BATCH))
    return jax.shard_map(
        per_device,
        mesh=finer,
        in_specs=placed,
        out_specs=(P(None, SEQ_BATCH), P(None, SEQ_BATCH)),
        check_vma=False,
    )
```

profile of v0, /device:TPU:1, one launch (start us, length us, event | category | flops | bytes accessed | tf_op | source)
XLA Modules:
  0.0 118.5 jit_solution(17248735630217335933)
XLA Ops:
  0.6 0.0 copy-start.3
  0.6 0.0 copy-start.1
  0.7 0.0 copy-start.2
  0.7 0.0 copy-start
  0.7 0.7 mul.124
  1.4 6.7 %fusion = (f32[2,8192]{1,0:T(2,128)S(1)}, f32[2,8192]{1,0:T(2,128)S(1)}) fusion(bf16[2,8192,128]{2,1,0:T(8,128)(2,1)} %param.7, f32[128]{0:T(128)S(1)} %mul.124), kind=kLoop, calls=%fused_computation.2 | loop fusion | flops 10452992 | bytes 4325888 | tf_op jit(solution)/shard_map/reduce_sum | solution.py:95
  8.0 0.7 pad_maximum_fusion
  8.7 11.9 %all-to-all-start = ((f32[32,4,256]{2,1,0:T(4,128)}), f32[32,4,256]{2,1,0:T(4,128)S(1)}, u32[]{:S(2)}, u32[]{:S(2)}) async-start(f32[32,4,256]{2,1,0:T(4,128)} %bitcast.1), calls=%async_computation | async-start | bytes 262144 | tf_op jit(solution)/shard_map/all_to_all | solution.py:22
  20.6 0.1 convert_compare_fusion
  20.7 0.0 copy-done.3
  20.8 9.0 %all-to-all-done = f32[32,4,256]{2,1,0:T(4,128)S(1)} async-done(((f32[32,4,256]{2,1,0:T(4,128)}), f32[32,4,256]{2,1,0:T(4,128)S(1)}, u32[]{:S(2)}, u32[]{:S(2)}) %all-to-all-start) | async-done | bytes 131104 | tf_op jit(solution)/shard_map/all_to_all | solution.py:22
  29.8 0.1 slice_reduce_fusion.1
  29.9 0.1 slice.115
  30.0 1.3 %collective-permute-start = (f32[2]{0:T(128)S(1)}, f32[2]{0:T(128)S(1)}, u32[]{:S(2)}, u32[]{:S(2)}) collective-permute-start(f32[2]{0:T(128)S(1)} %slice_reduce_fusion.1), channel_id=1, source_target_pairs={{8,0},{16,8},{24,16},{32,24},{40,32},{48,40},{56,48},{64,56},{72,6... | collective-permute-start | bytes 32 | tf_op jit(solution)/shard_map/ppermute | solution.py:36
  31.3 3.0 %collective-permute-done = f32[2]{0:T(128)S(1)} collective-permute-done((f32[2]{0:T(128)S(1)}, f32[2]{0:T(128)S(1)}, u32[]{:S(2)}, u32[]{:S(2)}) %collective-permute-start) | collective-permute-done | bytes 40 | tf_op jit(solution)/shard_map/ppermute | solution.py:36
  34.3 0.1 copy.15
  34.4 0.0 copy-done.1
  34.4 0.0 copy-done.2
  34.4 0.1 fusion.18
  34.5 0.7 fusion.2
  35.2 0.1 slice_reduce_fusion
  35.3 0.6 broadcast_in_dim.55
  35.9 5.2 %all-to-all-start.1 = ((f32[32,2,2]{2,1,0:T(2,128)}), f32[32,2,2]{2,1,0:T(2,128)S(1)}, u32[]{:S(2)}, u32[]{:S(2)}) async-start(f32[32,2,2]{2,1,0:T(2,128)} %broadcast_in_dim.55), calls=%async_computation.1 | async-start | bytes 65536 | tf_op jit(solution)/shard_map/all_to_all | solution.py:41
  41.1 8.8 %all-to-all-done.1 = f32[32,2,2]{2,1,0:T(2,128)S(1)} async-done(((f32[32,2,2]{2,1,0:T(2,128)}), f32[32,2,2]{2,1,0:T(2,128)S(1)}, u32[]{:S(2)}, u32[]{:S(2)}) %all-to-all-start.1) | async-done | bytes 544 | tf_op jit(solution)/shard_map/all_to_all | solution.py:41
  49.9 0.1 copy.16
  50.0 0.1 copy.17
  50.1 0.1 slice.99
  50.2 0.1 slice.94
  50.3 0.1 slice.91
  50.4 0.1 slice.96
  50.5 0.1 slice.100
  50.6 0.1 slice.92
  50.7 0.1 slice.95
  50.8 0.1 slice.97
  50.9 0.1 slice.101
  51.0 0.1 slice.104
  51.1 0.1 slice.102
  51.2 0.1 slice.98
  51.3 0.1 slice.103
  51.4 0.1 slice.106
  51.5 0.1 slice.105
  51.6 0.1 slice.108
  51.7 0.1 slice.107
  51.8 0.1 slice.110
  51.9 0.1 slice.109
  52.0 0.1 slice.112
  52.1 0.2 add_reduce_fusion
  52.3 0.7 compare_select_fusion
  53.0 0.6 fusion.20
  53.6 7.6 %all-reduce.2 = (f32[]{:T(128)}, f32[]{:T(128)}, f32[]{:T(128)}) all-reduce(f32[]{:T(128)} %get-tuple-element.5, f32[]{:T(128)} %get-tuple-element.24, f32[]{:T(128)} %get-tuple-element.4), channel_id=1, replica_groups=mesh['seq_0'=4,'seq_1'=8,'batch_0'=4,'batch_1'=2] {'seq_0'}, use_global_device_ids=true, to_apply=%region_14.15 | all-reduce | flops 3 | bytes 24 | tf_op jit(solution)/shard_map/psum | solution.py:87
  61.1 11.8 %all-reduce = (f32[]{:T(128)}, f32[]{:T(128)}, f32[]{:T(128)}) all-reduce(f32[]{:T(128)} %get-tuple-element.12, f32[]{:T(128)} %get-tuple-element.13, f32[]{:T(128)} %get-tuple-element.14), channel_id=1, replica_groups=mesh['seq_0'=4,'seq_1'=8,'batch_0'=4,'batch_1'=2] {'seq_1'}, use_global_device_ids=true, to_apply=%region_15.16 | all-reduce | flops 3 | bytes 24 | tf_op jit(solution)/shard_map/psum | solution.py:87
  72.9 9.7 %all-reduce.1 = (f32[]{:T(128)}, f32[]{:T(128)}, f32[]{:T(128)}) all-reduce(f32[]{:T(128)} %get-tuple-element.6, f32[]{:T(128)} %get-tuple-element.7, f32[]{:T(128)} %get-tuple-element.8), channel_id=1, replica_groups=mesh['seq_0'=4,'seq_1'=8,'batch_0'=4,'batch_1'=2] {'batch_0'}, use_global_device_ids=true, to_apply=%region_16.17 | all-reduce | flops 3 | bytes 24 | tf_op jit(solution)/shard_map/psum | solution.py:87
  82.6 14.5 %all-reduce.3 = (f32[]{:T(128)}, f32[]{:T(128)}, f32[]{:T(128)}) all-reduce(f32[]{:T(128)} %get-tuple-element.9, f32[]{:T(128)} %get-tuple-element.10, f32[]{:T(128)} %get-tuple-element.11), channel_id=1, replica_groups=mesh['seq_0'=4,'seq_1'=8,'batch_0'=4,'batch_1'=2] {'batch_1'}, use_global_device_ids=true, to_apply=%region_17.18 | all-reduce | flops 3 | bytes 24 | tf_op jit(solution)/shard_map/psum | solution.py:87
  99.8 0.1 fusion.13
  99.9 0.1 all_to_all.36
  99.9 0.6 copy.18
  100.6 3.6 %all-to-all-start.2 = ((f32[2,8,32]{2,0,1:T(2,128)}), f32[2,8,32]{2,0,1:T(2,128)S(1)}, u32[]{:S(2)}, u32[]{:S(2)}) async-start(f32[2,8,32]{2,0,1:T(2,128)} %copy.18), calls=%async_computation.2 | async-start | bytes 16384 | tf_op jit(solution)/shard_map/all_to_all | solution.py:137
  104.1 0.1 all_to_all.40
  104.2 0.6 copy.19
  104.8 4.0 %all-to-all-done.2 = f32[2,8,32]{2,0,1:T(2,128)S(1)} async-done(((f32[2,8,32]{2,0,1:T(2,128)}), f32[2,8,32]{2,0,1:T(2,128)S(1)}, u32[]{:S(2)}, u32[]{:S(2)}) %all-to-all-start.2) | async-done | bytes 2080 | tf_op jit(solution)/shard_map/all_to_all | solution.py:137
  108.8 3.9 %all-to-all-start.3 = ((f32[2,8,32]{2,0,1:T(2,128)}), f32[2,8,32]{2,0,1:T(2,128)S(1)}, u32[]{:S(2)}, u32[]{:S(2)}) async-start(f32[2,8,32]{2,0,1:T(2,128)} %copy.19), calls=%async_computation.3 | async-start | bytes 16384 | tf_op jit(solution)/shard_map/all_to_all | solution.py:138
  112.7 4.6 %all-to-all-done.3 = f32[2,8,32]{2,0,1:T(2,128)S(1)} async-done(((f32[2,8,32]{2,0,1:T(2,128)}), f32[2,8,32]{2,0,1:T(2,128)S(1)}, u32[]{:S(2)}, u32[]{:S(2)}) %all-to-all-start.3) | async-done | bytes 2080 | tf_op jit(solution)/shard_map/all_to_all | solution.py:138
  117.4 0.6 copy.31
  118.0 0.6 copy.32
  (16 shorter events, 0.2 us)
Async XLA Ops:
  0.6 20.1 %copy-start.3 = (f32[2]{0:T(128)S(1)}, f32[2]{0:T(128)}, u32[]{:S(2)}) copy-start(f32[2]{0:T(128)} %param.13) | copy-start | bytes 28
  0.6 33.8 %copy-start.1 = (f32[2,256]{1,0:T(2,128)S(1)}, f32[2,256]{1,0:T(2,128)}, u32[]{:S(2)}) copy-start(f32[2,256]{1,0:T(2,128)} %param.10) | copy-start | bytes 6148
  0.7 33.7 %copy-start.2 = (s32[2,256]{1,0:T(2,128)S(1)}, s32[2,256]{1,0:T(2,128)}, u32[]{:S(2)}) copy-start(s32[2,256]{1,0:T(2,128)} %param.11) | copy-start | bytes 6148
  0.7 33.7 %copy-start = (s32[2]{0:T(128)S(1)}, s32[2]{0:T(128)}, u32[]{:S(2)}) copy-start(s32[2]{0:T(128)} %param.12) | copy-start | bytes 28
  8.7 21.0 %all-to-all-start = ((f32[32,4,256]{2,1,0:T(4,128)}), f32[32,4,256]{2,1,0:T(4,128)S(1)}, u32[]{:S(2)}, u32[]{:S(2)}) async-start(f32[32,4,256]{2,1,0:T(4,128)} %bitcast.1), calls=%async_computation | async-start | bytes 262144 | tf_op jit(solution)/shard_map/all_to_all | solution.py:22
  30.0 4.3 %collective-permute-start = (f32[2]{0:T(128)S(1)}, f32[2]{0:T(128)S(1)}, u32[]{:S(2)}, u32[]{:S(2)}) collective-permute-start(f32[2]{0:T(128)S(1)} %slice_reduce_fusion.1), channel_id=1, source_target_pairs={{8,0},{16,8},{24,16},{32,24},{40,32},{48,40},{56,48},{64,56},{72,6... | collective-permute-start | bytes 32 | tf_op jit(solution)/shard_map/ppermute | solution.py:36
  35.9 13.9 %all-to-all-start.1 = ((f32[32,2,2]{2,1,0:T(2,128)}), f32[32,2,2]{2,1,0:T(2,128)S(1)}, u32[]{:S(2)}, u32[]{:S(2)}) async-start(f32[32,2,2]{2,1,0:T(2,128)} %broadcast_in_dim.55), calls=%async_computation.1 | async-start | bytes 65536 | tf_op jit(solution)/shard_map/all_to_all | solution.py:41
  100.6 8.2 %all-to-all-start.2 = ((f32[2,8,32]{2,0,1:T(2,128)}), f32[2,8,32]{2,0,1:T(2,128)S(1)}, u32[]{:S(2)}, u32[]{:S(2)}) async-start(f32[2,8,32]{2,0,1:T(2,128)} %copy.18), calls=%async_computation.2 | async-start | bytes 16384 | tf_op jit(solution)/shard_map/all_to_all | solution.py:137
  108.8 8.6 %all-to-all-start.3 = ((f32[2,8,32]{2,0,1:T(2,128)}), f32[2,8,32]{2,0,1:T(2,128)S(1)}, u32[]{:S(2)}, u32[]{:S(2)}) async-start(f32[2,8,32]{2,0,1:T(2,128)} %copy.19), calls=%async_computation.3 | async-start | bytes 16384 | tf_op jit(solution)/shard_map/all_to_all | solution.py:138
where the time goes:
time: 119 us
  blocking collectives  43.6 us (37%)
  waiting for transfers between devices  29.3 us (25%)
  starting transfers between devices  25.8 us (22%)
  other arithmetic  9.9 us (8%)
  local copies, waits for them, and re-layouts  5.74 us (5%)
  between operations  3.44 us (3%)
    psum x4, blocking collectives, one_axis_at_a_time(): array = lax.psum(array, axis)  43.6 us
    all_to_all x1, starting transfers between devices, sent_and_summed(): lax.all_to_all(cut_along(array, dim, devices), axis, 0, 0, tiled=True)  11.9 us
    all_to_all x1, waiting for transfers between devices, sent_and_summed(): lax.all_to_all(cut_along(array, dim, devices), axis, 0, 0, tiled=True)  8.98 us
    all_to_all x1, waiting for transfers between devices, sent_to_all(): lax.all_to_all(jnp.broadcast_to(array[None], (devices, *array.shape)), ax...  8.76 us
    reduce_sum x1, other arithmetic, per_device(): part_squares = jnp.sum(wide_rows * wide_rows, -1)  6.65 us
    all_to_all x1, starting transfers between devices, sent_to_all(): lax.all_to_all(jnp.broadcast_to(array[None], (devices, *array.shape)), ax...  5.16 us
    all_to_all x1, waiting for transfers between devices, per_device(): lax.all_to_all(returns, BATCH, split_axis=1, concat_axis=0, tiled=True)  4.64 us
    all_to_all x1, waiting for transfers between devices, per_device(): lax.all_to_all(whitened, BATCH, split_axis=1, concat_axis=0, tiled=True)  3.96 us
  transfers between devices with their start and end apart: 5, of which 5 were waited for; matrix products, arithmetic and copies ran while one was open for 1% of the time, Pallas kernels for 0%

commit v1 on v0

--- a/solution.py
+++ b/solution.py
@@ -84,7 +84,7 @@
 
 def one_axis_at_a_time(array, axes):
     for axis in axes:
-        array = lax.psum(array, axis)
+        array = jnp.sum(lax.all_gather(array, axis), axis=0)
     return array
 
 

time: 119 us -> 143 us (1.20)
  local copies, waits for them, and re-layouts: 5.74 us -> 25.1 us
  other arithmetic: 9.9 us -> 17.5 us
  blocking collectives: 43.6 us -> 40.9 us
    psum x4 -> x0, blocking collectives: 43.6 us -> none  [one_axis_at_a_time(): array = lax.psum(array, axis)]
    unnamed x0 -> x4, blocking collectives: none -> 40.9 us
    unnamed x10 -> x46, local copies, waits for them, and re-layouts: 1.21 us -> 20.6 us
    reduce_sum x0 -> x12, other arithmetic: none -> 7.45 us  [one_axis_at_a_time(): array = jnp.sum(lax.all_gather(array, axis), axis=0)]
where the time goes in v1:
time: 143 us; the launch traced here: 142 us
  blocking collectives  40.9 us (29%)
  waiting for transfers between devices  28.7 us (20%)
  starting transfers between devices  25.8 us (18%)
  local copies, waits for them, and re-layouts  25.1 us (18%)
  other arithmetic  17.5 us (12%)
  between operations  3.6 us (3%)
    unnamed x4, blocking collectives  40.9 us
    unnamed x46, local copies, waits for them, and re-layouts  20.6 us
    all_to_all x1, starting transfers between devices, sent_and_summed(): lax.all_to_all(cut_along(array, dim, devices), axis, 0, 0, tiled=True)  11.9 us
    all_to_all x1, waiting for transfers between devices, sent_and_summed(): lax.all_to_all(cut_along(array, dim, devices), axis, 0, 0, tiled=True)  8.98 us
    all_to_all x1, waiting for transfers between devices, sent_to_all(): lax.all_to_all(jnp.broadcast_to(array[None], (devices, *array.shape)), ax...  8.13 us
    reduce_sum x12, other arithmetic, one_axis_at_a_time(): array = jnp.sum(lax.all_gather(array, axis), axis=0)  7.45 us
    reduce_sum x1, other arithmetic, per_device(): part_squares = jnp.sum(wide_rows * wide_rows, -1)  6.65 us
    all_to_all x1, starting transfers between devices, sent_to_all(): lax.all_to_all(jnp.broadcast_to(array[None], (devices, *array.shape)), ax...  5.16 us
  transfers between devices with their start and end apart: 5, of which 5 were waited for; matrix products, arithmetic and copies ran while one was open for 1% of the time, Pallas kernels for 0%

profile of v1, /device:TPU:1, one launch (start us, length us, event | category | flops | bytes accessed | tf_op | source)
XLA Modules:
  0.0 142.3 jit_solution(13265880173990722360)
XLA Ops:
  0.7 0.7 mul.124
  1.4 6.7 %fusion = (f32[2,8192]{1,0:T(2,128)S(1)}, f32[2,8192]{1,0:T(2,128)S(1)}) fusion(bf16[2,8192,128]{2,1,0:T(8,128)(2,1)} %param.7, f32[128]{0:T(128)S(1)} %mul.124), kind=kLoop, calls=%fused_computation.2 | loop fusion | flops 10452992 | bytes 4325888 | tf_op jit(solution)/shard_map/reduce_sum | solution.py:95
  8.1 0.7 pad_maximum_fusion
  8.8 11.9 %all-to-all-start = ((f32[32,4,256]{2,1,0:T(4,128)}), f32[32,4,256]{2,1,0:T(4,128)S(1)}, u32[]{:S(2)}, u32[]{:S(2)}) async-start(f32[32,4,256]{2,1,0:T(4,128)} %bitcast.1), calls=%async_computation | async-start | bytes 262144 | tf_op jit(solution)/shard_map/all_to_all | solution.py:22
  20.8 9.0 %all-to-all-done = f32[32,4,256]{2,1,0:T(4,128)S(1)} async-done(((f32[32,4,256]{2,1,0:T(4,128)}), f32[32,4,256]{2,1,0:T(4,128)S(1)}, u32[]{:S(2)}, u32[]{:S(2)}) %all-to-all-start) | async-done | bytes 131104 | tf_op jit(solution)/shard_map/all_to_all | solution.py:22
  29.9 0.1 slice_reduce_fusion.1
  30.1 1.3 collective-permute-start
  31.4 3.0 %collective-permute-done = f32[2]{0:T(128)S(1)} collective-permute-done((f32[2]{0:T(128)S(1)}, f32[2]{0:T(128)S(1)}, u32[]{:S(2)}, u32[]{:S(2)}) %collective-permute-start) | collective-permute-done | bytes 40 | tf_op jit(solution)/shard_map/ppermute | solution.py:36
  34.5 0.7 fusion.2
  35.2 0.1 slice_reduce_fusion
  35.4 0.6 broadcast_in_dim.55
  36.0 5.2 %all-to-all-start.1 = ((f32[32,2,2]{2,1,0:T(2,128)}), f32[32,2,2]{2,1,0:T(2,128)S(1)}, u32[]{:S(2)}, u32[]{:S(2)}) async-start(f32[32,2,2]{2,1,0:T(2,128)} %broadcast_in_dim.55), calls=%async_computation.1 | async-start | bytes 65536 | tf_op jit(solution)/shard_map/all_to_all | solution.py:41
  41.2 0.6 dynamic-slice
  41.8 8.1 %all-to-all-done.1 = f32[32,2,2]{2,1,0:T(2,128)S(1)} async-done(((f32[32,2,2]{2,1,0:T(2,128)}), f32[32,2,2]{2,1,0:T(2,128)S(1)}, u32[]{:S(2)}, u32[]{:S(2)}) %all-to-all-start.1) | async-done | bytes 544 | tf_op jit(solution)/shard_map/all_to_all | solution.py:41
  50.1 0.1 slice.99
  50.3 0.1 slice.94
  50.4 0.1 slice.91
  50.5 0.1 slice.96
  50.6 0.1 slice.100
  51.0 0.1 slice.101
  51.3 0.1 slice.98
  51.8 0.1 slice.107
  52.1 0.2 add_reduce_fusion
  52.3 0.7 compare_select_fusion
  53.0 0.7 fusion.20
  53.7 1.4 dynamic-update-slice
  55.1 1.4 %dynamic-update-slice.8 = f32[4]{0:T(128)S(1)} dynamic-update-slice(f32[4]{0:T(128)S(1)} %broadcast.69.clone.1, f32[1]{0:T(128)} %bitcast.20, u32[]{:T(128)} %bitcast.9) | dynamic-update-slice | bytes 12
  56.5 1.4 dynamic-update-slice.4
  57.9 0.6 dynamic-slice.1
  58.5 6.8 %all-reduce.14 = (f32[4]{0:T(128)S(1)}, f32[4]{0:T(128)S(1)}, f32[4]{0:T(128)S(1)}) all-reduce(f32[4]{0:T(128)S(1)} %dynamic-update-slice.8, f32[4]{0:T(128)S(1)} %dynamic-update-slice.4, f32[4]{0:T(128)S(1)} %dynamic-update-slice), channel_id=1, replica_groups=mesh['seq_0'=4,'seq_1'=8,'batch_0'=4,'batch_1'=2] {'seq_0'}, use_global_device_ids=true, to_apply=%add.8 | all-reduce | flops 12 | bytes 96
  65.4 0.7 reduce_sum.166
  66.0 0.6 reduce_sum.171
  66.6 1.4 %dynamic-update-slice.1 = f32[8]{0:T(128)S(1)} dynamic-update-slice(f32[8]{0:T(128)S(1)} %broadcast.68.clone.2, f32[1]{0:T(128)} %bitcast.10, u32[]{:T(128)} %bitcast.11) | dynamic-update-slice | bytes 12
  68.1 1.4 dynamic-update-slice.5
  69.5 0.6 reduce_sum.176
  70.1 1.4 dynamic-update-slice.9
  71.5 0.6 dynamic-slice.2
  72.1 11.1 %all-reduce.12 = (f32[8]{0:T(128)S(1)}, f32[8]{0:T(128)S(1)}, f32[8]{0:T(128)S(1)}) all-reduce(f32[8]{0:T(128)S(1)} %dynamic-update-slice.9, f32[8]{0:T(128)S(1)} %dynamic-update-slice.5, f32[8]{0:T(128)S(1)} %dynamic-update-slice.1), channel_id=1, replica_groups=mesh['seq_0'=4,'seq_1'=8,'batch_0'=4,'batch_1'=2] {'seq_1'}, use_global_device_ids=true, to_apply=%add.9 | all-reduce | flops 24 | bytes 192
  83.2 0.7 reduce_sum.167
  83.8 0.6 reduce_sum.172
  84.4 1.4 %dynamic-update-slice.2 = f32[4]{0:T(128)S(1)} dynamic-update-slice(f32[4]{0:T(128)S(1)} %broadcast.69.clone.5, f32[1]{0:T(128)} %bitcast.12, u32[]{:T(128)} %bitcast.13) | dynamic-update-slice | bytes 12
  85.9 1.4 dynamic-update-slice.6
  87.3 0.6 reduce_sum.177
  87.9 1.4 dynamic-update-slice.10
  89.3 0.6 dynamic-slice.3
  89.9 8.7 %all-reduce.13 = (f32[4]{0:T(128)S(1)}, f32[4]{0:T(128)S(1)}, f32[4]{0:T(128)S(1)}) all-reduce(f32[4]{0:T(128)S(1)} %dynamic-update-slice.10, f32[4]{0:T(128)S(1)} %dynamic-update-slice.6, f32[4]{0:T(128)S(1)} %dynamic-update-slice.2), channel_id=1, replica_groups=mesh['seq_0'=4,'seq_1'=8,'batch_0'=4,'batch_1'=2] {'batch_0'}, use_global_device_ids=true, to_apply=%add.10 | all-reduce | flops 12 | bytes 96
  98.6 0.7 reduce_sum.168
  99.3 0.6 reduce_sum.173
  99.9 1.4 %dynamic-update-slice.3 = f32[2]{0:T(128)S(1)} dynamic-update-slice(f32[2]{0:T(128)S(1)} %broadcast.70.clone.2, f32[1]{0:T(128)} %bitcast.14, u32[]{:T(128)} %bitcast.15) | dynamic-update-slice | bytes 12
  101.3 1.4 dynamic-update-slice.7
  102.7 0.6 reduce_sum.178
  103.3 1.4 dynamic-update-slice.11
  104.7 14.3 %all-reduce.15 = (f32[2]{0:T(128)S(1)}, f32[2]{0:T(128)S(1)}, f32[2]{0:T(128)S(1)}) all-reduce(f32[2]{0:T(128)S(1)} %dynamic-update-slice.11, f32[2]{0:T(128)S(1)} %dynamic-update-slice.7, f32[2]{0:T(128)S(1)} %dynamic-update-slice.3), channel_id=1, replica_groups=mesh['seq_0'=4,'seq_1'=8,'batch_0'=4,'batch_1'=2] {'batch_1'}, use_global_device_ids=true, to_apply=%add.11 | all-reduce | flops 6 | bytes 48
  119.0 0.6 reduce_sum.169
  119.6 0.6 reduce_sum.174
  121.5 0.6 reduce_sum.179
  123.7 0.6 copy.18
  124.3 3.6 %all-to-all-start.2 = ((f32[2,8,32]{2,0,1:T(2,128)}), f32[2,8,32]{2,0,1:T(2,128)S(1)}, u32[]{:S(2)}, u32[]{:S(2)}) async-start(f32[2,8,32]{2,0,1:T(2,128)} %copy.18), calls=%async_computation.2 | async-start | bytes 16384 | tf_op jit(solution)/shard_map/all_to_all | solution.py:137
  127.9 0.6 copy.19
  128.6 4.0 %all-to-all-done.2 = f32[2,8,32]{2,0,1:T(2,128)S(1)} async-done(((f32[2,8,32]{2,0,1:T(2,128)}), f32[2,8,32]{2,0,1:T(2,128)S(1)}, u32[]{:S(2)}, u32[]{:S(2)}) %all-to-all-start.2) | async-done | bytes 2080 | tf_op jit(solution)/shard_map/all_to_all | solution.py:137
  132.5 3.9 %all-to-all-start.3 = ((f32[2,8,32]{2,0,1:T(2,128)}), f32[2,8,32]{2,0,1:T(2,128)S(1)}, u32[]{:S(2)}, u32[]{:S(2)}) async-start(f32[2,8,32]{2,0,1:T(2,128)} %copy.19), calls=%async_computation.3 | async-start | bytes 16384 | tf_op jit(solution)/shard_map/all_to_all | solution.py:138
  136.4 4.6 %all-to-all-done.3 = f32[2,8,32]{2,0,1:T(2,128)S(1)} async-done(((f32[2,8,32]{2,0,1:T(2,128)}), f32[2,8,32]{2,0,1:T(2,128)S(1)}, u32[]{:S(2)}, u32[]{:S(2)}) %all-to-all-start.3) | async-done | bytes 2080 | tf_op jit(solution)/shard_map/all_to_all | solution.py:138
  141.1 0.6 copy.56
  141.7 0.6 copy.57
  (64 shorter events, 2.1 us)
Async XLA Ops:
  0.6 40.6 %copy-start.7 = (u32[256]{0:T(256)S(1)}, u32[256]{0:T(256)}, u32[]{:S(2)}) copy-start(u32[256]{0:T(256)} %constant.45) | copy-start | bytes 3076
  0.6 57.3 %copy-start.6 = (u32[256]{0:T(256)S(1)}, u32[256]{0:T(256)}, u32[]{:S(2)}) copy-start(u32[256]{0:T(256)} %constant.50) | copy-start | bytes 3076
  0.7 70.8 %copy-start.5 = (u32[256]{0:T(256)S(1)}, u32[256]{0:T(256)}, u32[]{:S(2)}) copy-start(u32[256]{0:T(256)} %constant.55) | copy-start | bytes 3076
  0.7 88.6 %copy-start.4 = (u32[256]{0:T(256)S(1)}, u32[256]{0:T(256)}, u32[]{:S(2)}) copy-start(u32[256]{0:T(256)} %constant.60) | copy-start | bytes 3076
  0.7 20.1 %copy-start.3 = (f32[2]{0:T(128)S(1)}, f32[2]{0:T(128)}, u32[]{:S(2)}) copy-start(f32[2]{0:T(128)} %param.13) | copy-start | bytes 28
  0.7 33.8 %copy-start.1 = (f32[2,256]{1,0:T(2,128)S(1)}, f32[2,256]{1,0:T(2,128)}, u32[]{:S(2)}) copy-start(f32[2,256]{1,0:T(2,128)} %param.10) | copy-start | bytes 6148
  0.7 33.8 %copy-start.2 = (s32[2,256]{1,0:T(2,128)S(1)}, s32[2,256]{1,0:T(2,128)}, u32[]{:S(2)}) copy-start(s32[2,256]{1,0:T(2,128)} %param.11) | copy-start | bytes 6148
  0.7 33.8 %copy-start = (s32[2]{0:T(128)S(1)}, s32[2]{0:T(128)}, u32[]{:S(2)}) copy-start(s32[2]{0:T(128)} %param.12) | copy-start | bytes 28
  8.8 21.0 %all-to-all-start = ((f32[32,4,256]{2,1,0:T(4,128)}), f32[32,4,256]{2,1,0:T(4,128)S(1)}, u32[]{:S(2)}, u32[]{:S(2)}) async-start(f32[32,4,256]{2,1,0:T(4,128)} %bitcast.1), calls=%async_computation | async-start | bytes 262144 | tf_op jit(solution)/shard_map/all_to_all | solution.py:22
  30.1 4.3 %collective-permute-start = (f32[2]{0:T(128)S(1)}, f32[2]{0:T(128)S(1)}, u32[]{:S(2)}, u32[]{:S(2)}) collective-permute-start(f32[2]{0:T(128)S(1)} %slice_reduce_fusion.1), channel_id=1, source_target_pairs={{8,0},{16,8},{24,16},{32,24},{40,32},{48,40},{56,48},{64,56},{72,6... | collective-permute-start | bytes 32 | tf_op jit(solution)/shard_map/ppermute | solution.py:36
  36.0 13.9 %all-to-all-start.1 = ((f32[32,2,2]{2,1,0:T(2,128)}), f32[32,2,2]{2,1,0:T(2,128)S(1)}, u32[]{:S(2)}, u32[]{:S(2)}) async-start(f32[32,2,2]{2,1,0:T(2,128)} %broadcast_in_dim.55), calls=%async_computation.1 | async-start | bytes 65536 | tf_op jit(solution)/shard_map/all_to_all | solution.py:41
  124.3 8.2 %all-to-all-start.2 = ((f32[2,8,32]{2,0,1:T(2,128)}), f32[2,8,32]{2,0,1:T(2,128)S(1)}, u32[]{:S(2)}, u32[]{:S(2)}) async-start(f32[2,8,32]{2,0,1:T(2,128)} %copy.18), calls=%async_computation.2 | async-start | bytes 16384 | tf_op jit(solution)/shard_map/all_to_all | solution.py:137
  132.5 8.6 %all-to-all-start.3 = ((f32[2,8,32]{2,0,1:T(2,128)}), f32[2,8,32]{2,0,1:T(2,128)S(1)}, u32[]{:S(2)}, u32[]{:S(2)}) async-start(f32[2,8,32]{2,0,1:T(2,128)} %copy.19), calls=%async_computation.3 | async-start | bytes 16384 | tf_op jit(solution)/shard_map/all_to_all | solution.py:138
